TPU v7x, 16 devices: a whole 2x2x2 slice. The times are simulated.
16 devices in a mesh: rep: 1, dp: 16 (over x, y, z, core).
Axes of the slice: x: 2, y: 2, z: 2, core: 2. Of those that a mesh axis runs over, the one named last changes fastest.
Arguments:
- a: bfloat16 [16, 4, 4096, 1280], P(('rep', 'dp'))
- g: bfloat16 [16, 4, 4096, 3072], P(('rep', 'dp'))
Outputs:
- output: bfloat16 [4, 1280, 3072], P('rep')
All inputs are finite; a program needn't handle non-finite values.
Results may differ from a plain program's by a relative error of at most 0.012.
Values are sent between devices in bfloat16 or wider.
A program may use at most 2 GiB of HBM per device.

v0:
```python
import jax
import jax.numpy as jnp


def solution(mesh):
    groups = mesh.shape["rep"]

    def step(a, g):
        a, g = (t.reshape(groups, -1, *t.shape[1:]) for t in (a, g))
        sums = jnp.einsum("rsntd,rsntf->rndf", a, g, preferred_element_type=jnp.float32)
        return sums.astype(jnp.bfloat16).reshape(-1, *sums.shape[2:])

    return step
```

profile of v0, /device:TPU:0, one launch (start us, length us, event | category | flops | bytes accessed | tf_op | source)
XLA Modules:
  0.0 715.6 jit_solution(1243721832896321391)
XLA Ops:
  0.0 142.3 %fusion = f32[4,1280,3072]{2,1,0:T(8,128)} fusion(bf16[1,4,4096,3072]{3,2,1,0:T(8,128)(2,1)} %param.1, bf16[1,4,4096,1280]{3,2,1,0:T(8,128)(2,1)} %param), kind=kOutput, calls=%fused_computation | convolution fusion | flops 128849018880 | bytes 205520896 | tf_op jit(solution)/rsntd,rsntf->rndf/dot_general | solution.py:10
  142.3 573.3 %all-reduce.2 = bf16[4,1280,3072]{2,1,0:T(8,128)(2,1)} all-reduce(f32[4,1280,3072]{2,1,0:T(8,128)} %fusion), channel_id=1, replica_groups=mesh['axis_0'=16] {'axis_0'}, use_global_device_ids=true, to_apply=%add.clone | all-reduce | flops 15728640 | bytes 94371840 | tf_op jit(solution)/rsntd,rsntf->rndf/dot_general | solution.py:10
where the time goes:
time: 716 us
  blocking collectives  573 us (80%)
  matrix products  142 us (20%)
    dot_general x1, blocking collectives, step(): jnp.einsum('rsntd,rsntf->rndf', a, g, preferred_element_type=jnp.float32)  573 us
    dot_general x1, matrix products, step(): jnp.einsum('rsntd,rsntf->rndf', a, g, preferred_element_type=jnp.float32)  142 us

commit v1 on v0

v1 whole, which is shorter than its diff:
```python
import functools

import jax
import jax.numpy as jnp
from jax import lax
from jax.experimental import pallas as pl
from jax.experimental.pallas import tpu as pltpu
from jax.sharding import PartitionSpec as P

COLS = 256
CHUNK = 512
LAG = 3


def kernel(a_ref, g_ref, out_ref, at, gb, stg, own, ag, s0s, r1s, r2s, r3s, r1r, r2r, r3r,
           s0_send, s0_recv, r1_send, r1_recv, r2_send, r2_recv, r3_send, r3_recv,
           ag1_recv, ag2_recv, ag3_recv, ag1_send, ag2_send, ag3_send, core_send, core_recv, out_sem, g_sem, a_sem):
    _, mats, tokens, d = a_ref.shape
    per = g_ref.shape[3] // COLS
    units = mats * per
    chunks = tokens // CHUNK
    half, q1, q2, q3 = d // 2, d // 4, d // 8, d // 16
    f32, bf16 = jnp.float32, jnp.bfloat16

    me = lax.axis_index("dp")
    bit = {k: lax.rem(me // k, 2) for k in (8, 4, 2, 1)}
    peer = {k: me + k - 2 * k * bit[k] for k in (8, 4, 2, 1)}
    c = bit[1]

    barrier = pltpu.get_barrier_semaphore()
    for k in (8, 4, 2, 1):
        pl.semaphore_signal(barrier, inc=1, device_id={"dp": peer[k]}, device_id_type=pl.DeviceIdType.MESH)
    pl.semaphore_wait(barrier, 4)

    def dims(w):
        r = lax.rem(w, 3)

        def sel(x, y, z):
            return jnp.where(r == 0, x, jnp.where(r == 1, y, z))

        b = (sel(bit[8], bit[4], bit[2]), sel(bit[4], bit[2], bit[8]), sel(bit[2], bit[8], bit[4]))
        p = (sel(peer[8], peer[4], peer[2]), sel(peer[4], peer[2], peer[8]), sel(peer[2], peer[8], peer[4]))
        return b, p

    def rows(start, size):
        return pl.ds(pl.multiple_of(start, 16), size)

    def remote(src, dst, send, recv, to):
        return pltpu.make_async_remote_copy(src_ref=src, dst_ref=dst, send_sem=send, recv_sem=recv,
                                            device_id={"dp": to}, device_id_type=pl.DeviceIdType.MESH)

    def load_g(t):
        n, j = t // per, lax.rem(t, per)
        slot = lax.rem(t, 2)
        return pltpu.make_async_copy(
            g_ref.at[0, n, :, pl.ds(pl.multiple_of(j * COLS, COLS), COLS)], gb.at[slot], g_sem.at[slot])

    def load_a(n, i):
        slot = lax.rem(i, 2)
        return pltpu.make_async_copy(
            a_ref.at[0, n, pl.ds(pl.multiple_of(i * CHUNK, CHUNK), CHUNK), :], stg.at[slot], a_sem.at[slot])

    def transpose(n, i):
        at[lax.rem(n, 2), :, pl.ds(pl.multiple_of(i * CHUNK, CHUNK), CHUNK)] = stg[lax.rem(i, 2)].T

    def dot(t, row):
        return jnp.dot(at[lax.rem(t // per, 2), rows(row, half), :], gb[lax.rem(t, 2)], preferred_element_type=f32)

    def s0(w):
        k = lax.rem(w, 3)
        return remote(s0s.at[k], ag.at[w], s0_send.at[k], s0_recv.at[lax.rem(w, 4)], peer[1])

    def r1(w):
        k, m = lax.rem(w, 4), lax.rem(w, 6)
        return remote(r1s.at[k], r1r.at[m], r1_send.at[k], r1_recv.at[m], dims(w)[1][0])

    def r2(w):
        k, m = lax.rem(w, 4), lax.rem(w, 6)
        return remote(r2s.at[k], r2r.at[m], r2_send.at[k], r2_recv.at[m], dims(w)[1][1])

    def r3(w):
        k, m = lax.rem(w, 4), lax.rem(w, 6)
        return remote(r3s.at[k], r3r.at[m], r3_send.at[k], r3_recv.at[m], dims(w)[1][2])

    def g1(v):
        b, p = dims(v)
        part = ag.at[v, rows(b[0] * q1 + b[1] * q2 + b[2] * q3, q3)]
        return remote(part, part, ag1_send, ag1_recv.at[v], p[2])

    def g2(v):
        b, p = dims(v)
        part = ag.at[v, rows(b[0] * q1 + b[1] * q2, q2)]
        return remote(part, part, ag2_send, ag2_recv.at[v], p[1])

    def g3(v):
        b, p = dims(v)
        part = ag.at[v, rows(b[0] * q1, q1)]
        return remote(part, part, ag3_send, ag3_recv.at[v], p[0])

    def target(v):
        return out_ref.at[v // per, rows(c * half, half), pl.ds(pl.multiple_of(lax.rem(v, per) * COLS, COLS), COLS)]

    def finish(v):
        remote(ag.at[v], target(v), core_send, core_recv, peer[1]).start()
        pltpu.make_async_copy(ag.at[v], target(v), out_sem).start()

    def add1(w):
        k = lax.rem(w, 8)
        (b1, _, _), _ = dims(w)
        give, keep = rows((1 - b1) * q1, q1), rows(b1 * q1, q1)
        r1s[lax.rem(w, 4)] = (own[k, give] + ag[w, give].astype(f32)).astype(bf16)
        own[k, keep] = own[k, keep] + ag[w, keep].astype(f32)

    def add2(w):
        k, m = lax.rem(w, 8), lax.rem(w, 6)
        (b1, b2, _), _ = dims(w)
        give, keep = (1 - b2) * q2, b2 * q2
        r2s[lax.rem(w, 4)] = (own[k, rows(b1 * q1 + give, q2)] + r1r[m, rows(give, q2)].astype(f32)).astype(bf16)
        kept = rows(b1 * q1 + keep, q2)
        own[k, kept] = own[k, kept] + r1r[m, rows(keep, q2)].astype(f32)

    def add3(w):
        k, m = lax.rem(w, 8), lax.rem(w, 6)
        (b1, b2, b3), _ = dims(w)
        base = b1 * q1 + b2 * q2
        give, keep = (1 - b3) * q3, b3 * q3
        r3s[lax.rem(w, 4)] = (own[k, rows(base + give, q3)] + r2r[m, rows(give, q3)].astype(f32)).astype(bf16)
        kept = rows(base + keep, q3)
        own[k, kept] = own[k, kept] + r2r[m, rows(keep, q3)].astype(f32)

    def add4(w):
        k, m = lax.rem(w, 8), lax.rem(w, 6)
        (b1, b2, b3), _ = dims(w)
        kept = rows(b1 * q1 + b2 * q2 + b3 * q3, q3)
        ag[w, kept] = (own[k, kept] + r3r[m].astype(f32)).astype(bf16)

    def step(t, compute, guard):
        def when(cond, f):
            if guard:
                pl.when(cond)(f)
            else:
                f()

        def live(lag):
            return jnp.logical_and(t >= lag, t - lag < units)

        if compute:
            n, j = t // per, lax.rem(t, per)
            more = n + 1 < mats

            @pl.when(t + 1 < units)
            def _():
                load_g(t + 1).start()

            @pl.when(jnp.logical_and(more, j == 0))
            def _():
                load_a(n + 1, 0).start()

            @pl.when(jnp.logical_and(more, j + 1 < chunks))
            def _():
                load_a(n + 1, j + 1).start()

            @pl.when(jnp.logical_and(more, j < chunks))
            def _():
                load_a(n + 1, j).wait()
                transpose(n + 1, j)

            when(t >= 3, lambda: s0(t - 3).wait_send())
            load_g(t).wait()
            s0s[lax.rem(t, 3)] = dot(t, (1 - c) * half).astype(bf16)
            s0(t).start()

        def waits1():
            s0(t - 1).wait_recv()

        when(live(1), waits1)
        when(live(5), lambda: r1(t - 5).wait_send())
        when(live(3), lambda: r1(t - 3).wait_recv())
        when(live(7), lambda: r2(t - 7).wait_send())
        when(live(5), lambda: r2(t - 5).wait_recv())
        when(live(9), lambda: r3(t - 9).wait_send())
        when(live(7), lambda: r3(t - 7).wait_recv())
        when(live(1), lambda: add1(t - 1))
        when(live(3), lambda: add2(t - 3))
        when(live(5), lambda: add3(t - 5))
        when(live(7), lambda: add4(t - 7))
        if compute:
            own[lax.rem(t, 8)] = dot(t, c * half)
        when(live(1), lambda: r1(t - 1).start())
        when(live(3), lambda: r2(t - 3).start())
        when(live(5), lambda: r3(t - 5).start())

        def gather2():
            g1(t - 9 - LAG).wait_recv()
            g2(t - 9 - LAG).start()

        def gather3():
            g2(t - 9 - 2 * LAG).wait_recv()
            g3(t - 9 - 2 * LAG).start()

        def gather4():
            g3(t - 9 - 3 * LAG).wait_recv()
            finish(t - 9 - 3 * LAG)

        when(live(9), lambda: g1(t - 9).start())
        when(live(9 + LAG), gather2)
        when(live(9 + 2 * LAG), gather3)
        when(live(9 + 3 * LAG), gather4)

    def loop(lo, hi, compute, guard):
        def body(t, _):
            step(t, compute, guard)
            return 0

        lax.fori_loop(lo, hi, body, 0)

    load_g(0).start()
    load_a(0, 0).start()

    def first(i, _):
        @pl.when(i + 1 < chunks)
        def _():
            load_a(0, i + 1).start()

        load_a(0, i).wait()
        transpose(0, i)
        return 0

    lax.fori_loop(0, chunks, first, 0)

    deep = 9 + 3 * LAG
    loop(0, deep, True, True)
    loop(deep, units, True, False)
    loop(units, units + deep, False, True)

    for k in range(units - 3, units):
        s0(k).wait_send()

    def all_of(size, sem):
        whole = ag.at[pl.ds(0, units * size // half)]
        pltpu.make_async_copy(whole, whole, sem).wait()

    all_of(q3, ag1_send)
    all_of(q2, ag2_send)
    all_of(q1, ag3_send)
    all_of(half, core_send)
    all_of(half, core_recv)
    all_of(half, out_sem)


def solution(mesh):
    def step(a, g):
        _, mats, tokens, d = a.shape
        ff = g.shape[3]
        units = mats * ff // COLS
        half = d // 2
        bf16 = jnp.bfloat16
        dma = pltpu.SemaphoreType.DMA
        return pl.pallas_call(
            kernel,
            out_shape=jax.ShapeDtypeStruct((mats, d, ff), bf16),
            in_specs=[pl.BlockSpec(memory_space=pl.ANY)] * 2,
            out_specs=pl.BlockSpec(memory_space=pl.ANY),
            scratch_shapes=[
                pltpu.VMEM((2, d, tokens), bf16),
                pltpu.VMEM((2, tokens, COLS), bf16),
                pltpu.VMEM((2, CHUNK, d), bf16),
                pltpu.VMEM((8, half, COLS), jnp.float32),
                pltpu.VMEM((units, half, COLS), bf16),
                pltpu.VMEM((3, half, COLS), bf16),
                pltpu.VMEM((4, half // 2, COLS), bf16),
                pltpu.VMEM((4, half // 4, COLS), bf16),
                pltpu.VMEM((4, half // 8, COLS), bf16),
                pltpu.VMEM((6, half // 2, COLS), bf16),
                pltpu.VMEM((6, half // 4, COLS), bf16),
                pltpu.VMEM((6, half // 8, COLS), bf16),
                dma((3,)), dma((4,)), dma((4,)), dma((6,)), dma((4,)), dma((6,)), dma((4,)), dma((6,)),
                dma((units,)), dma((units,)), dma((units,)), dma, dma, dma, dma, dma, dma, dma((2,)), dma((2,)),
            ],
            compiler_params=pltpu.CompilerParams(
                collective_id=0, has_side_effects=True, vmem_limit_bytes=64 * 1024 * 1024 - 65536),
            name="grads",
        )(a, g)

    return jax.shard_map(step, mesh=mesh, in_specs=(P(("rep", "dp")),) * 2, out_specs=P("rep"), check_vma=False)
```

time: 716 us -> 374 us (0.52)
  blocking collectives: 573 us -> 0 us
  Pallas kernels: 0 us -> 352 us
  matrix products: 142 us -> 0 us
  local copies, waits for them, and re-layouts: 0 us -> 21.5 us
    dot_general x1 -> x0, blocking collectives: 573 us -> none  [step(): jnp.einsum('rsntd,rsntf->rndf', a, g, preferred_element_type=jnp.float32)]
    pallas_call x0 -> x1, Pallas kernels: none -> 352 us  [step(): pl.pallas_call(kernel, out_shape=jax.ShapeDtypeStruct((mats, d, ff), bf16...]
    dot_general x1 -> x0, matrix products: 142 us -> none  [step(): jnp.einsum('rsntd,rsntf->rndf', a, g, preferred_element_type=jnp.float32)]
    unnamed x0 -> x1, local copies, waits for them, and re-layouts: none -> 21.5 us
where the time goes in v1:
time: 374 us
  Pallas kernels  352 us (94%)
  local copies, waits for them, and re-layouts  21.5 us (6%)
    pallas_call x1, Pallas kernels, step(): pl.pallas_call(kernel, out_shape=jax.ShapeDtypeStruct((mats, d, ff), bf16...  352 us
    unnamed x1, local copies, waits for them, and re-layouts  21.5 us

profile of v1, /device:TPU:0, one launch (start us, length us, event | category | flops | bytes accessed | tf_op | source)
XLA Modules:
  0.0 373.8 jit_solution(1982148929902546982)
XLA Ops:
  0.0 352.4 %grads.1 = bf16[4,1280,3072]{2,1,0:T(8,128)(2,1)} custom-call(bf16[1,4,4096,1280]{3,2,1,0:T(8,128)(2,1)} %a_ref.1, bf16[1,4,4096,3072]{3,2,1,0:T(8,128)(2,1)} %g_ref.1), custom_call_target="tpu_custom_call" | custom-call | tf_op jit(solution)/shard_map/grads/pallas_call | solution.py:259
  352.4 21.5 %copy.4 = bf16[4,1280,3072]{2,1,0:T(8,128)(2,1)} copy(bf16[4,1280,3072]{2,1,0:T(8,128)(2,1)} %grads.1) | data formatting | bytes 62914560

commit v2 on v0

v2 whole, which is shorter than its diff:
```python
import functools

import jax
import jax.numpy as jnp
from jax import lax
from jax.experimental import pallas as pl
from jax.experimental.pallas import tpu as pltpu
from jax.sharding import PartitionSpec as P

COLS = 256
CHUNK = 512
LAG = 3
E1, E2, E3, E4, G1 = 1, 3, 5, 6, 6
TURN = 3
RING = 6
LAND = 12
PIECE = 80
HELD = 12
ORDERS = ((8, 4, 2), (4, 2, 8), (2, 8, 4))


def mod(x, y):
    return x % y if isinstance(x, int) else lax.rem(x, y)


def kernel(a_ref, g_ref, out_ref, at, gb, stg, own, ag, s0s, r1s, r2s, r3s, r1r, r2r, r3r,
           s0_send, s0_recv, r1_send, r1_recv, r2_send, r2_recv, r3_send, r3_recv,
           ag1_recv, ag2_recv, ag3_recv, ag1_send, ag2_send, ag3_send, core_send, core_recv, out_sem, g_sem, a_sem):
    _, mats, tokens, d = a_ref.shape
    per = g_ref.shape[3] // COLS
    units = mats * per
    chunks = tokens // CHUNK
    half, q1, q2, q3 = d // 2, d // 4, d // 8, d // 16
    f32, bf16 = jnp.float32, jnp.bfloat16

    me = lax.axis_index("dp")
    bit = {k: mod(me // k, 2) for k in (8, 4, 2, 1)}
    peer = {k: me + k - 2 * k * bit[k] for k in (8, 4, 2, 1)}
    c = bit[1]

    barrier = pltpu.get_barrier_semaphore()
    for k in (8, 4, 2, 1):
        pl.semaphore_signal(barrier, inc=1, device_id={"dp": peer[k]}, device_id_type=pl.DeviceIdType.MESH)
    pl.semaphore_wait(barrier, 4)

    class Unit:
        def __init__(self, s, i, lag):
            back, self.r = divmod(i - lag, TURN)
            self.w = TURN * s + (i - lag)
            self.s = s + back
            self.b = [bit[k] for k in ORDERS[self.r]]
            self.p = [peer[k] for k in ORDERS[self.r]]

        def slot(self, size):
            return self.r if size == TURN else TURN * mod(self.s + 8, size // TURN) + self.r

        def place(self):
            return self.s // (per // TURN), TURN * mod(self.s + 8 * per, per // TURN) + self.r

    def rows(start, size):
        return pl.ds(pl.multiple_of(start, 16), size)

    def remote(src, dst, send, recv, to):
        return pltpu.make_async_remote_copy(src_ref=src, dst_ref=dst, send_sem=send, recv_sem=recv,
                                            device_id={"dp": to}, device_id_type=pl.DeviceIdType.MESH)

    def load_g(u):
        n, j = u.place()
        slot = mod(u.w, 2)
        return pltpu.make_async_copy(
            g_ref.at[0, n, :, pl.ds(pl.multiple_of(j * COLS, COLS), COLS)], gb.at[slot], g_sem.at[slot])

    def load_a(n, i):
        slot = mod(i, 2)
        return pltpu.make_async_copy(
            a_ref.at[0, n, pl.ds(pl.multiple_of(i * CHUNK, CHUNK), CHUNK), :], stg.at[slot], a_sem.at[slot])

    def transpose(n, i):
        at[mod(n, 2), :, pl.ds(pl.multiple_of(i * CHUNK, CHUNK), CHUNK)] = stg[mod(i, 2)].T

    def dot(u, row):
        return jnp.dot(
            at[mod(u.place()[0], 2), rows(row, half), :], gb[mod(u.w, 2)], preferred_element_type=f32)

    def s0(u):
        k, m = u.slot(TURN), u.slot(LAND)
        return remote(s0s.at[k], ag.at[u.w], s0_send.at[k], s0_recv.at[m], peer[1])

    def r1(u):
        m, l = u.slot(RING), u.slot(LAND)
        return remote(r1s.at[m], r1r.at[l], r1_send.at[m], r1_recv.at[l], u.p[0])

    def r2(u):
        m, l = u.slot(RING), u.slot(LAND)
        return remote(r2s.at[m], r2r.at[l], r2_send.at[m], r2_recv.at[l], u.p[1])

    def r3(u):
        m, l = u.slot(RING), u.slot(LAND)
        return remote(r3s.at[m], r3r.at[l], r3_send.at[m], r3_recv.at[l], u.p[2])

    def g1(u):
        part = ag.at[u.w, rows(u.b[0] * q1 + u.b[1] * q2 + u.b[2] * q3, q3)]
        return remote(part, part, ag1_send, ag1_recv.at[u.w], u.p[2])

    def g2(u):
        part = ag.at[u.w, rows(u.b[0] * q1 + u.b[1] * q2, q2)]
        return remote(part, part, ag2_send, ag2_recv.at[u.w], u.p[1])

    def g3(u):
        part = ag.at[u.w, rows(u.b[0] * q1, q1)]
        return remote(part, part, ag3_send, ag3_recv.at[u.w], u.p[0])

    def finish(u):
        n, j = u.place()
        to = out_ref.at[n, rows(c * half, half), pl.ds(pl.multiple_of(j * COLS, COLS), COLS)]
        remote(ag.at[u.w], to, core_send, core_recv, peer[1]).start()
        pltpu.make_async_copy(ag.at[u.w], to, out_sem).start()

    def pieces(size, f):
        for i in range(size // PIECE):
            f(i * PIECE)

    def add(u, base, size, got, bit, send):
        k = u.slot(HELD)
        give, keep = (1 - bit) * size, bit * size

        def piece(off):
            send[rows(off, PIECE)] = (
                own[k, rows(base + give + off, PIECE)] + got[rows(give + off, PIECE)].astype(f32)).astype(bf16)
            kept = rows(base + keep + off, PIECE)
            own[k, kept] = own[k, kept] + got[rows(keep + off, PIECE)].astype(f32)

        pieces(size, piece)

    def add1(u):
        add(u, 0, q1, ag.at[u.w], u.b[0], r1s.at[u.slot(RING)])

    def add2(u):
        add(u, u.b[0] * q1, q2, r1r.at[u.slot(LAND)], u.b[1], r2s.at[u.slot(RING)])

    def add3(u):
        add(u, u.b[0] * q1 + u.b[1] * q2, q3, r2r.at[u.slot(LAND)], u.b[2], r3s.at[u.slot(RING)])

    def add4(u):
        k, m = u.slot(HELD), u.slot(LAND)
        base = u.b[0] * q1 + u.b[1] * q2 + u.b[2] * q3

        def piece(off):
            kept = rows(base + off, PIECE)
            ag[u.w, kept] = (own[k, kept] + r3r[m, rows(off, PIECE)].astype(f32)).astype(bf16)

        pieces(q3, piece)

    def gather1(u):
        g1(u).start()

    def gather2(u):
        g1(u).wait_recv()
        g2(u).start()

    def gather3(u):
        g2(u).wait_recv()
        g3(u).start()

    def gather4(u):
        g3(u).wait_recv()
        finish(u)

    def step(s, i, guard):
        t = TURN * s + i

        def do(lag, f):
            def run():
                f(Unit(s, i, lag))

            if guard:
                pl.when(jnp.logical_and(t >= lag, t - lag < units))(run)
            else:
                run()

        u = Unit(s, i, 0)
        n, j = u.place()
        more = n + 1 < mats

        @pl.when(t + 1 < units)
        def _():
            load_g(Unit(s, i, -1)).start()

        if i == 0:
            @pl.when(jnp.logical_and(more, j == 0))
            def _():
                load_a(n + 1, 0).start()

        @pl.when(jnp.logical_and(more, j + 1 < chunks))
        def _():
            load_a(n + 1, j + 1).start()

        @pl.when(jnp.logical_and(more, j < chunks))
        def _():
            load_a(n + 1, j).wait()
            transpose(n + 1, j)

        do(TURN, lambda u: s0(u).wait_send())
        load_g(u).wait()

        s0s[u.slot(TURN)] = dot(u, (1 - c) * half).astype(bf16)
        own[u.slot(HELD)] = dot(u, c * half)
        s0(u).start()

        def halve(lag, before, add, copy):
            do(lag, lambda u: before(u).wait_recv())
            do(lag + RING, lambda u: copy(u).wait_send())
            do(lag, add)
            do(lag, lambda u: copy(u).start())

        halve(E1, s0, add1, r1)
        halve(E2, r1, add2, r2)
        halve(E3, r2, add3, r3)
        do(E4, lambda u: r3(u).wait_recv())
        do(E4, add4)
        do(G1, gather1)
        do(G1 + LAG, gather2)
        do(G1 + 2 * LAG, gather3)
        do(G1 + 3 * LAG, gather4)

    def loop(lo, hi, guard):
        def body(s, _):
            for i in range(TURN):
                step(s, i, guard)
            return 0

        lax.fori_loop(lo, hi, body, 0)

    load_g(Unit(0, 0, 0)).start()
    load_a(0, 0).start()

    def first(i, _):
        @pl.when(i + 1 < chunks)
        def _():
            load_a(0, i + 1).start()

        load_a(0, i).wait()
        transpose(0, i)
        return 0

    lax.fori_loop(0, chunks, first, 0)

    deep = G1 + 3 * LAG
    turns = units // TURN
    full = -(-max(deep, E3 + RING) // TURN)
    loop(0, full, True)
    loop(full, turns, False)

    def last(lag):
        return units - lag

    at_stage = [last(lag) for lag in (E1, E2, E3, E4, G1, G1 + LAG, G1 + 2 * LAG, G1 + 3 * LAG)]
    ahead = units
    while at_stage[-1] < units:
        todo = []
        for lo in at_stage:
            todo.append([Unit(w // TURN, w % TURN, 0) for w in range(lo, ahead)])
            ahead = lo
        for u in todo[0]:
            s0(u).wait_recv()
            r1(Unit(u.s - RING // TURN, u.r, 0)).wait_send()
            add1(u)
            r1(u).start()
        for u in todo[1]:
            r1(u).wait_recv()
            r2(Unit(u.s - RING // TURN, u.r, 0)).wait_send()
            add2(u)
            r2(u).start()
        for u in todo[2]:
            r2(u).wait_recv()
            r3(Unit(u.s - RING // TURN, u.r, 0)).wait_send()
            add3(u)
            r3(u).start()
        for u in todo[3]:
            r3(u).wait_recv()
            add4(u)
        for u in todo[4] + todo[3]:
            gather1(u)
        for u in todo[5]:
            gather2(u)
        for u in todo[6]:
            gather3(u)
        for u in todo[7]:
            gather4(u)
        at_stage = [units] + at_stage[:3] + [at_stage[2]] + at_stage[4:7]
        ahead = units
    for u in [Unit(w // TURN, w % TURN, 0) for w in range(units - RING, units)]:
        r1(u).wait_send()
        r2(u).wait_send()
        r3(u).wait_send()

    for i in range(TURN):
        s0(Unit(turns - 1, i, 0)).wait_send()

    def all_of(size, sem):
        whole = ag.at[pl.ds(0, units * size // half)]
        pltpu.make_async_copy(whole, whole, sem).wait()

    all_of(q3, ag1_send)
    all_of(q2, ag2_send)
    all_of(q1, ag3_send)
    all_of(half, core_send)
    all_of(half, core_recv)
    all_of(half, out_sem)


def solution(mesh):
    def step(a, g):
        _, mats, tokens, d = a.shape
        ff = g.shape[3]
        units = mats * ff // COLS
        half = d // 2
        bf16 = jnp.bfloat16
        dma = pltpu.SemaphoreType.DMA
        return pl.pallas_call(
            kernel,
            out_shape=jax.ShapeDtypeStruct((mats, d, ff), bf16),
            in_specs=[pl.BlockSpec(memory_space=pl.ANY)] * 2,
            out_specs=pl.BlockSpec(memory_space=pl.ANY),
            scratch_shapes=[
                pltpu.VMEM((2, d, tokens), bf16),
                pltpu.VMEM((2, tokens, COLS), bf16),
                pltpu.VMEM((2, CHUNK, d), bf16),
                pltpu.VMEM((HELD, half, COLS), jnp.float32),
                pltpu.VMEM((units, half, COLS), bf16),
                pltpu.VMEM((3, half, COLS), bf16),
                pltpu.VMEM((RING, half // 2, COLS), bf16),
                pltpu.VMEM((RING, half // 4, COLS), bf16),
                pltpu.VMEM((RING, half // 8, COLS), bf16),
                pltpu.VMEM((LAND, half // 2, COLS), bf16),
                pltpu.VMEM((LAND, half // 4, COLS), bf16),
                pltpu.VMEM((LAND, half // 8, COLS), bf16),
                dma((TURN,)), dma((LAND,)), dma((RING,)), dma((LAND,)), dma((RING,)), dma((LAND,)), dma((RING,)), dma((LAND,)),
                dma((units,)), dma((units,)), dma((units,)), dma, dma, dma, dma, dma, dma, dma((2,)), dma((2,)),
            ],
            compiler_params=pltpu.CompilerParams(
                collective_id=0, has_side_effects=True, vmem_limit_bytes=64 * 1024 * 1024 - 65536),
            name="grads",
        )(a, g)

    return jax.shard_map(step, mesh=mesh, in_specs=(P(("rep", "dp")),) * 2, out_specs=P("rep"), check_vma=False)
```

time: 716 us -> 262 us (0.37)
  blocking collectives: 573 us -> 0 us
  Pallas kernels: 0 us -> 240 us
  matrix products: 142 us -> 0 us
  local copies, waits for them, and re-layouts: 0 us -> 21.5 us
    dot_general x1 -> x0, blocking collectives: 573 us -> none  [step(): jnp.einsum('rsntd,rsntf->rndf', a, g, preferred_element_type=jnp.float32)]
    pallas_call x0 -> x1, Pallas kernels: none -> 240 us  [step(): pl.pallas_call(kernel, out_shape=jax.ShapeDtypeStruct((mats, d, ff), bf16...]
    dot_general x1 -> x0, matrix products: 142 us -> none  [step(): jnp.einsum('rsntd,rsntf->rndf', a, g, preferred_element_type=jnp.float32)]
    unnamed x0 -> x1, local copies, waits for them, and re-layouts: none -> 21.5 us
where the time goes in v2:
time: 262 us
  Pallas kernels  240 us (92%)
  local copies, waits for them, and re-layouts  21.5 us (8%)
    pallas_call x1, Pallas kernels, step(): pl.pallas_call(kernel, out_shape=jax.ShapeDtypeStruct((mats, d, ff), bf16...  240 us
    unnamed x1, local copies, waits for them, and re-layouts  21.5 us

profile of v2, /device:TPU:0, one launch (start us, length us, event | category | flops | bytes accessed | tf_op | source)
XLA Modules:
  0.0 261.7 jit_solution(4643042929188117622)
XLA Ops:
  0.0 240.2 %grads.1 = bf16[4,1280,3072]{2,1,0:T(8,128)(2,1)} custom-call(bf16[1,4,4096,1280]{3,2,1,0:T(8,128)(2,1)} %a_ref.1, bf16[1,4,4096,3072]{3,2,1,0:T(8,128)(2,1)} %g_ref.1), custom_call_target="tpu_custom_call" | custom-call | tf_op jit(solution)/shard_map/grads/pallas_call | solution.py:320
  240.2 21.5 %copy.4 = bf16[4,1280,3072]{2,1,0:T(8,128)(2,1)} copy(bf16[4,1280,3072]{2,1,0:T(8,128)(2,1)} %grads.1) | data formatting | bytes 62914560
